TPU v7x, 8 devices: a whole 2x2x1 slice. The times are simulated.
8 devices in a mesh: dp: 1 (over z), tp: 2 (over y), fsdp: 2 (over x), cp: 2 (over core).
Axes of the slice: x: 2, y: 2, z: 1, core: 2. Of those that a mesh axis runs over, the one named last changes fastest.
Arguments:
- hidden: bfloat16 [6, 3072, 3584], P(('dp', 'fsdp'), 'cp')
- positions: int32 [6, 3072], P(('dp', 'fsdp'), 'cp')
- attn_gain: float32 [3584], replicated
- w_query: bfloat16 [3584, 28, 128], P(('fsdp', 'cp'), 'tp')
- w_key: bfloat16 [3584, 4, 128], P(('fsdp', 'cp'), 'tp')
- w_value: bfloat16 [3584, 4, 128], P(('fsdp', 'cp'), 'tp')
- w_out: bfloat16 [28, 128, 3584], P('tp', None, ('fsdp', 'cp'))
- mlp_gain: float32 [3584], replicated
- w_gate: bfloat16 [3584, 18944], P(('fsdp', 'cp'), 'tp')
- w_up: bfloat16 [3584, 18944], P(('fsdp', 'cp'), 'tp')
- w_down: bfloat16 [18944, 3584], P('tp', ('fsdp', 'cp'))
Outputs:
- output: bfloat16 [6, 3072, 3584], P(('dp', 'fsdp'), 'cp')
All inputs are finite; a program needn't handle non-finite values.
Results may differ from a plain program's by a relative error of at most 0.0123897.
Values are sent between devices in bfloat16 or wider.
A program may use at most 1 GiB of HBM per device.

v0:
```python
import jax
import jax.numpy as jnp
from jax import lax
from jax.sharding import PartitionSpec as P, NamedSharding

ROPE_THETA = 500000.0
NORM_EPS = 1e-5
QBLOCK = 128
GROUP_AXES = ('fsdp', 'cp')


def rms_norm(hidden_f32, gain):
    mean_sq = jnp.mean(hidden_f32 * hidden_f32, axis=-1, keepdims=True)
    return (hidden_f32 * lax.rsqrt(mean_sq + NORM_EPS) * gain).astype(jnp.bfloat16)


def rope_tables(positions, head_dim):
    inv_freq = ROPE_THETA ** (-jnp.arange(0, head_dim, 2, dtype=jnp.float32) / head_dim)
    angles = positions.astype(jnp.float32)[..., None] * inv_freq
    return jnp.cos(angles)[..., None, :], jnp.sin(angles)[..., None, :]


def apply_rope(projected, rope_cos, rope_sin):
    half_dim = projected.shape[-1] // 2
    first_half = projected[..., :half_dim]
    second_half = projected[..., half_dim:]
    return jnp.concatenate([first_half * rope_cos - second_half * rope_sin, second_half * rope_cos + first_half * rope_sin], axis=-1)


def attention(queries, keys, values, q_pos, k_pos):
    n_seqs, tokens, kv_heads, group_size, head_dim = queries.shape
    n_blocks = tokens // QBLOCK
    q_blocks = queries.reshape(n_seqs * n_blocks, QBLOCK, kv_heads, group_size, head_dim)
    pos_blocks = q_pos.reshape(n_seqs * n_blocks, QBLOCK)
    seq_ids = jnp.arange(n_seqs * n_blocks) // n_blocks
    score_scale = head_dim ** -0.5

    def one_block(block_args):
        q_blk, qpos_blk, seq_id = block_args
        k_seq = lax.dynamic_index_in_dim(keys, seq_id, 0, keepdims=False)
        v_seq = lax.dynamic_index_in_dim(values, seq_id, 0, keepdims=False)
        kpos_seq = lax.dynamic_index_in_dim(k_pos, seq_id, 0, keepdims=False)
        scores = jnp.einsum('qkgd,skd->kgqs', q_blk, k_seq, preferred_element_type=jnp.float32) * score_scale
        visible = qpos_blk[:, None] >= kpos_seq[None, :]
        scores = jnp.where(visible, scores, -jnp.inf)
        row_max = jnp.max(scores, axis=-1, keepdims=True)
        probs = jnp.exp(scores - row_max)
        row_sum = jnp.sum(probs, axis=-1)
        weighted = jnp.einsum('kgqs,skd->qkgd', probs.astype(jnp.bfloat16), v_seq, preferred_element_type=jnp.float32)
        return (weighted / jnp.transpose(row_sum, (2, 0, 1))[..., None]).astype(jnp.bfloat16)

    mixed = lax.map(one_block, (q_blocks, pos_blocks, seq_ids))
    return mixed.reshape(n_seqs, tokens, kv_heads * group_size, head_dim)


def solution(mesh):
    seq_spec = P(('dp', 'fsdp'), 'cp', None)
    pos_spec = P(('dp', 'fsdp'), 'cp')
    in_spec = P(GROUP_AXES, 'tp', None)
    out_spec = P('tp', None, GROUP_AXES)
    col_spec = P(GROUP_AXES, 'tp')
    row_spec = P('tp', GROUP_AXES)
    rep_spec = P(None)

    def layer_local(hidden, positions, attn_gain, w_query, w_key, w_value, w_out, mlp_gain, w_gate, w_up, w_down):
        n_seqs, tokens, d_model = hidden.shape
        kv_heads = w_key.shape[1]
        head_dim = w_key.shape[2]
        group_size = w_query.shape[1] // kv_heads
        hidden_f32 = hidden.astype(jnp.float32)
        normed = rms_norm(hidden_f32, attn_gain)
        rope_cos, rope_sin = rope_tables(positions, head_dim)
        full_query = lax.all_gather(w_query, GROUP_AXES, axis=0, tiled=True)
        full_key = lax.all_gather(w_key, GROUP_AXES, axis=0, tiled=True)
        full_value = lax.all_gather(w_value, GROUP_AXES, axis=0, tiled=True)
        queries = apply_rope(jnp.einsum('bsd,dhe->bshe', normed, full_query, preferred_element_type=jnp.float32), rope_cos, rope_sin).astype(jnp.bfloat16)
        keys = apply_rope(jnp.einsum('bsd,dhe->bshe', normed, full_key, preferred_element_type=jnp.float32), rope_cos, rope_sin).astype(jnp.bfloat16)
        values = jnp.einsum('bsd,dhe->bshe', normed, full_value, preferred_element_type=jnp.float32).astype(jnp.bfloat16)
        all_keys = lax.all_gather(keys, 'cp', axis=1, tiled=True)
        all_values = lax.all_gather(values, 'cp', axis=1, tiled=True)
        all_pos = lax.all_gather(positions, 'cp', axis=1, tiled=True)
        mixed = attention(queries.reshape(n_seqs, tokens, kv_heads, group_size, head_dim), all_keys, all_values, positions, all_pos)
        full_out = lax.all_gather(w_out, GROUP_AXES, axis=2, tiled=True)
        attn_part = jnp.einsum('bshe,hed->bsd', mixed, full_out, preferred_element_type=jnp.float32).astype(jnp.bfloat16)
        attn_out = lax.psum(attn_part, 'tp')
        mid_f32 = (hidden_f32 + attn_out.astype(jnp.float32)).astype(jnp.bfloat16).astype(jnp.float32)
        normed_mlp = rms_norm(mid_f32, mlp_gain)
        full_gate = lax.all_gather(w_gate, GROUP_AXES, axis=0, tiled=True)
        full_up = lax.all_gather(w_up, GROUP_AXES, axis=0, tiled=True)
        gate_proj = jnp.einsum('bsd,df->bsf', normed_mlp, full_gate, preferred_element_type=jnp.float32)
        up_proj = jnp.einsum('bsd,df->bsf', normed_mlp, full_up, preferred_element_type=jnp.float32)
        act_mlp = (jax.nn.silu(gate_proj) * up_proj).astype(jnp.bfloat16)
        full_down = lax.all_gather(w_down, GROUP_AXES, axis=1, tiled=True)
        down_part = jnp.einsum('bsf,fd->bsd', act_mlp, full_down, preferred_element_type=jnp.float32).astype(jnp.bfloat16)
        down_proj = lax.psum(down_part, 'tp')
        return (mid_f32 + down_proj.astype(jnp.float32)).astype(jnp.bfloat16)

    return jax.shard_map(layer_local, mesh=mesh, in_specs=(seq_spec, pos_spec, rep_spec, in_spec, in_spec, in_spec, out_spec, rep_spec, col_spec, col_spec, row_spec), out_specs=seq_spec, check_vma=False)
```

profile of v0, /device:TPU:0, one launch (start us, length us, event | category | flops | bytes accessed | tf_op | source)
XLA Modules:
  0.0 4762.0 jit_solution(17871218013544202255)
XLA Ops:
  32.6 17.7 fusion.60
  55.5 18.0 convolution_convert_fusion
  77.7 54.7 %all-gather.18.cloned.1.call-done = bf16[3584,14,128]{0,2,1:T(8,128)(2,1)} async-done(((bf16[896,14,128]{0,2,1:T(8,128)(2,1)}), bf16[3584,14,128]{0,2,1:T(8,128)(2,1)}) %all-gather.18.cloned.1.call-update) | async-done | bytes 12845072 | tf_op jit(solution)/shard_map/all_gather | solution.py:73
  132.4 70.0 %fusion.58 = f32[3,1536,14,128]{1,3,2,0:T(8,128)} fusion(bf16[3584,14,128]{0,2,1:T(8,128)(2,1)} %all-gather.18.cloned.1.call-done, bf16[3,1536,3584]{2,1,0:T(8,128)(2,1)} %param.13, f32[3584]{0:T(1024)S(1)} %copy-done.6, f32[3,1536]{1,0:T(4,128)S(1)} %add_rsqrt_fusion.1), kind=kOutput, calls=%fused_computation.54 | convolution fusion | flops 59256078336 | bytes 78938112 | tf_op jit(solution)/shard_map/bsd,dhe->bshe/dot_general | solution.py:76
  202.4 15.0 subtract_convert_fusion
  217.4 23.2 copy.22
  240.6 21.8 concatenate.14
  275.0 21.8 concatenate.15
  296.8 16.7 pad_maximum_fusion
  313.6 26.5 copy.26
  340.1 1338.6 %while.10 = (s32[]{:T(128)}, bf16[36,128,2,7,128]{4,1,0,3,2:T(8,128)(2,1)}, s32[36]{0:T(128)S(1)}, bf16[3,3072,2,128]{3,1,2,0:T(8,128)(2,1)}, s32[36,128]{1,0:T(...) while((s32[]{:T(128)}, ...), condition=%wide.region_4.5_spmd, body=%wide.region_1.4_spmd.sunk | while | flops 2879975936 | bytes 161687248 | solution.py:52
  363.1 13.0 fusion.89
  883.6 13.0 fusion.89
  995.2 13.0 fusion.89
  1032.3 13.0 fusion.89
  1181.0 13.0 fusion.89
  1218.2 13.0 fusion.89
  1441.4 13.0 fusion.89
  1552.9 13.0 fusion.89
  1590.1 13.0 fusion.89
  1664.5 13.0 fusion.89
  1678.7 68.0 %bitcast_convert_fusion = bf16[3,1536,3584]{2,1,0:T(8,128)(2,1)} fusion(bf16[3,1536,14,128]{3,1,0,2:T(8,128)(2,1)} %bitcast.133, bf16[14,128,3584]{2,1,0:T(8,128)(2,1)} %all-gather.20.cloned.1.call-done), kind=kOutput, calls=%fused_computation.47 | convolution fusion | flops 59206533120 | bytes 62390272 | tf_op jit(solution)/shard_map/bshe,hed->bsd/dot_general | solution.py:84
  1748.8 718.6 %all-reduce.3.cloned.1.call-done = bf16[3,1536,3584]{2,1,0:T(8,128)(2,1)} async-done(((bf16[3,1536,3584]{2,1,0:T(8,128)(2,1)}), bf16[3,1536,3584]{2,1,0:T(8,128)(2,1)}) %all-reduce.3.cloned.1.call-update) | async-done | bytes 33030160 | tf_op jit(solution)/shard_map/psum | solution.py:85
  2467.4 33.2 fusion.47
  2500.6 364.7 %all-gather.24.cloned.1.call-done = bf16[3584,9472]{1,0:T(8,128)(2,1)} async-done(((bf16[896,9472]{1,0:T(8,128)(2,1)}), bf16[3584,9472]{1,0:T(8,128)(2,1)}) %all-gather.24.cloned.1.call-update) | async-done | bytes 67895312 | tf_op jit(solution)/shard_map/all_gather | solution.py:89
  2865.3 353.0 %fusion.40 = f32[3,1536,9472]{2,1,0:T(8,128)} fusion(bf16[3584,9472]{1,0:T(8,128)(2,1)} %all-gather.24.cloned.1.call-done, bf16[3,1536,3584]{2,1,0:T(8,128)(2,1)} %get-tuple-element.81, f32[3584]{0:T(1024)S(1)} %copy-done.7, f32[3,1536]{1,0:T(4,128)S(1)} %add_rsqrt_fusion), kind=kOutput, calls=%fused_computation.36 | convolution fusion | flops 312927584256 | bytes 275546112 | tf_op jit(solution)/shard_map/bsd,df->bsf/dot_general | solution.py:91
  3218.3 44.9 all-gather.22.cloned.1.call-done
  3263.2 376.5 %multiply_convert_fusion = bf16[3,1536,9472]{2,1,0:T(8,128)(2,1)} fusion(f32[3,1536,9472]{2,1,0:T(8,128)} %fusion.40, bf16[3584,9472]{1,0:T(8,128)(2,1)} %all-gather.22.cloned.1.call-done, bf16[3,1536,3584]{2,1,0:T(8,128)(2,1)} %get-tuple-element.81, f32[3584]{0:T(1024)S(1)} %copy-done.7, f32[3,1536]{1,0:T(4,128)S(1)} %add_rsqrt_fusion), kind=kOutput, calls=%fused_computation.27 | convolution fusion | flops 313189466112 | bytes 362840064 | tf_op jit(solution)/shard_map/bsd,df->bsf/dot_general | solution.py:90
  3639.6 20.8 all-gather.26.cloned.1.call-done
  3660.4 341.8 %fusion.52 = bf16[3,1536,3584]{2,1,0:T(8,128)(2,1)} fusion(bf16[3,1536,9472]{2,1,0:T(8,128)(2,1)} %multiply_convert_fusion, bf16[9472,3584]{1,0:T(8,128)(2,1)} %all-gather.26.cloned.1.call-done), kind=kOutput, calls=%fused_computation.49 | convolution fusion | flops 312878039040 | bytes 188219392 | tf_op jit(solution)/shard_map/bsf,fd->bsd/dot_general | solution.py:94
  4002.2 720.7 %all-reduce.5.cloned.1.call-done = bf16[3,1536,3584]{2,1,0:T(8,128)(2,1)} async-done(((bf16[3,1536,3584]{2,1,0:T(8,128)(2,1)}), bf16[3,1536,3584]{2,1,0:T(8,128)(2,1)}) %all-reduce.5.cloned.1.call-update) | async-done | bytes 33030160 | tf_op jit(solution)/shard_map/psum | solution.py:95
  4722.9 32.3 fusion.50
  (445 shorter events, 1187.3 us)
Async XLA Ops:
  6.5 26.0 all-gather.14.cloned.1.call-start
  8.5 47.0 all-gather.10.cloned.1.call-start
  10.5 22.1 copy-start.6
  10.5 121.9 %all-gather.18.cloned.1.call-start = ((), (), s32[]{:S(2)}) async-start(), calls=%async_computation.4 | async-start | bytes 16056320 | tf_op jit(solution)/shard_map/all_gather | solution.py:73
  16.2 323.9 %all-gather.16.cloned.1.call-start = ((), (), s32[]{:S(2)}) async-start(), calls=%async_computation.3 | async-start | bytes 7077888 | tf_op jit(solution)/shard_map/all_gather | solution.py:79
  32.5 17.8 copy-start.1
  32.5 17.8 copy-start.3
  55.3 18.9 copy-start.5
  55.3 284.8 %all-gather.12.cloned.1.call-start = ((), (), s32[]{:S(2)}) async-start(), calls=%async_computation.1 | async-start | bytes 7077888 | tf_op jit(solution)/shard_map/all_gather | solution.py:80
  73.5 1605.2 %all-gather.20.cloned.1.call-start = ((), (), s32[]{:S(2)}) async-start(), calls=%async_computation.5 | async-start | bytes 16056320 | tf_op jit(solution)/shard_map/all_gather | solution.py:83
  74.1 2393.3 %all-reduce.3.cloned.1.call-start = ((), (), s32[]{:S(2)}) async-start(), calls=%async_computation.6 | async-start | bytes 66060288 | tf_op jit(solution)/shard_map/psum | solution.py:85
  132.4 70.0 %copy-start.2 = (f32[3,1536,64]{1,2,0:T(8,128)S(1)}, f32[3,1536,64]{1,2,0:T(8,128)}, u32[]{:S(2)}) copy-start(f32[3,1536,64]{1,2,0:T(8,128)} %copy-done.1) | copy-start | bytes 3538948
  132.4 70.0 %copy-start.4 = (f32[3,1536,64]{1,2,0:T(8,128)S(1)}, f32[3,1536,64]{1,2,0:T(8,128)}, u32[]{:S(2)}) copy-start(f32[3,1536,64]{1,2,0:T(8,128)} %copy-done.3) | copy-start | bytes 3538948
  313.6 26.5 copy-start.8
  350.7 7.9 copy-start
  387.9 7.9 copy-start
  499.4 7.9 copy-start
  573.7 7.9 copy-start
  759.6 7.9 copy-start
  796.8 7.9 copy-start
  833.9 7.9 copy-start
  871.1 7.9 copy-start
  908.3 7.9 copy-start
  982.7 7.9 copy-start
  1019.9 7.9 copy-start
  1057.0 7.9 copy-start
  1094.2 7.9 copy-start
  1746.7 1118.6 %all-gather.24.cloned.1.call-start = ((), (), s32[]{:S(2)}) async-start(), calls=%async_computation.8 | async-start | bytes 84869120 | tf_op jit(solution)/shard_map/all_gather | solution.py:89
  1747.4 1515.7 %all-gather.22.cloned.1.call-start = ((), (), s32[]{:S(2)}) async-start(), calls=%async_computation.7 | async-start | bytes 84869120 | tf_op jit(solution)/shard_map/all_gather | solution.py:88
  1748.2 1912.2 %all-gather.26.cloned.1.call-start = ((), (), s32[]{:S(2)}) async-start(), calls=%async_computation.9 | async-start | bytes 84869120 | tf_op jit(solution)/shard_map/all_gather | solution.py:93
  1748.8 1116.5 %copy-start.7 = (f32[3584]{0:T(1024)S(1)}, f32[3584]{0:T(1024)}, u32[]{:S(2)}) copy-start(f32[3584]{0:T(1024)} %param.20) | copy-start | bytes 43012
  1748.8 2974.1 %all-reduce.5.cloned.1.call-start = ((), (), s32[]{:S(2)}) async-start(), calls=%async_computation.10 | async-start | bytes 66060288 | tf_op jit(solution)/shard_map/psum | solution.py:95
  (23 other events, 181.4 us)
Sparse Core Ops, SparseCore 0:
  8.9 20.9 all-gather.13
  31.4 18.0 all-gather.9
  51.0 81.3 all-gather.17
  133.8 12.0 all-gather.15
  147.2 13.2 all-gather.11
  161.9 82.5 all-gather.19
  1746.8 720.5 all-reduce.2
  2469.0 396.2 all-gather.23
  2866.8 396.2 all-gather.21
  3264.5 395.8 all-gather.25
  4002.3 720.5 all-reduce.4
where the time goes:
time: 4780 us; the launch traced here: 4760 us
  waiting for transfers between devices  1930 us (40%)
  matrix products  1900 us (40%)
  local copies, waits for them, and re-layouts  517 us (11%)
  other arithmetic  332 us (7%)
  loops' own time  71.6 us (1%)
    psum x1, waiting for transfers between devices, layer_local(): down_proj = lax.psum(down_part, 'tp')  721 us
    psum x1, waiting for transfers between devices, layer_local(): attn_out = lax.psum(attn_part, 'tp')  719 us
    dot_general x36, matrix products, one_block(): jnp.einsum('kgqs,skd->qkgd', probs.astype(jnp.bfloat16), v_seq, preferred...  467 us
    dot_general x1, matrix products, layer_local(): jnp.einsum('bsd,df->bsf', normed_mlp, full_gate, preferred_element_type=j...  376 us
    all_gather x1, waiting for transfers between devices, layer_local(): full_up = lax.all_gather(w_up, GROUP_AXES, axis=0, tiled=True)  365 us
    dot_general x1, matrix products, layer_local(): jnp.einsum('bsd,df->bsf', normed_mlp, full_up, preferred_element_type=jnp...  353 us
    dot_general x1, matrix products, layer_local(): jnp.einsum('bsf,fd->bsd', act_mlp, full_down, preferred_element_type=jnp....  342 us
    while x72, local copies, waits for them, and re-layouts  284 us
  transfers between devices with their start and end apart: 11, of which 6 were waited for; matrix products, arithmetic and copies ran while one was open for 42% of the time, Pallas kernels for 0%

commit v1 on v0

v1 whole, which is shorter than its diff:
```python
import functools

import jax
import jax.numpy as jnp
from jax import lax
from jax.experimental import pallas as pl
from jax.experimental.pallas import tpu as pltpu
from jax.sharding import PartitionSpec as P


ROPE_THETA = 500000.0
NORM_EPS = 1e-5
HEAD = 128
LOG2E = 1.4426950408889634
GROUP_AXES = ('fsdp', 'cp')
VMEM_LIMIT = 66_500_000
ROWS = 384
F_CHUNKS = (10, 10, 10, 7)
F_UNIT = 256
D_CHUNKS = ((0, 3), (3, 4))
STEPS = (
    ('q', 0), ('a', 0), ('o', 0), ('q', 1), ('q', 2), ('a', 1), ('o', 1), ('a', 2), ('n', 0), ('o', 2),
    ('g', 0, 0, 1), ('g', 0, 1, 1), ('n', 1), ('g', 1, 0, 2), ('g', 0, 2, 1), ('g', 1, 2, 1), ('R', 0), ('n', 2),
    ('g', 1, 3, 1), ('d', 1, 0, 0, 7), ('g', 2, 0, 1), ('R2', 0), ('g', 0, 3, 1),
    ('d', 1, 1, 0, 3), ('d', 0, 1, 0, 3), ('d', 0, 0, 0, 7), ('R2', 1), ('g', 2, 1, 1),
    ('d', 0, 1, 3, 4), ('d', 1, 1, 3, 4), ('g', 2, 2, 2),
    ('d', 2, 0, 0, 2), ('d', 2, 1, 0, 3), ('d', 2, 0, 2, 5), ('f', 1, 0), ('d', 2, 1, 3, 4),
    ('f', 2, 0), ('f', 0, 0), ('f', 0, 1), ('f', 1, 1), ('f', 2, 1),
)


def cost(flops, bytes_accessed):
    return pl.CostEstimate(flops=int(flops), bytes_accessed=int(bytes_accessed), transcendentals=0)


def params(n_axes):
    return pltpu.CompilerParams(dimension_semantics=('arbitrary',) * n_axes, vmem_limit_bytes=VMEM_LIMIT)


def qkv_kernel(x_ref, gain_ref, w_ref, cos_ref, sin_ref, q_ref, kv_ref, normed, *, heads, kv_heads):
    rows = x_ref.shape[1]

    def norm(i, carry):
        part = pl.ds(i * 64, 64)
        x = x_ref[0, part, :].astype(jnp.float32)
        mean_sq = jnp.mean(x * x, axis=-1, keepdims=True)
        normed[part, :] = (x * lax.rsqrt(mean_sq + NORM_EPS) * gain_ref[...]).astype(jnp.bfloat16)
        return carry

    lax.fori_loop(0, rows // 64, norm, 0)
    cos = cos_ref[...]
    sin = sin_ref[...]
    for pair in range(w_ref.shape[1] // 256):
        y = jnp.dot(normed[...], w_ref[:, pair * 256:(pair + 1) * 256], preferred_element_type=jnp.float32)
        for half in range(2):
            head = 2 * pair + half
            yh = y[:, half * HEAD:(half + 1) * HEAD]
            if head < heads + kv_heads:
                yh = yh * cos + pltpu.roll(yh, HEAD // 2, 1) * sin
            if head < heads:
                q_ref[:, head * HEAD:(head + 1) * HEAD] = yh.astype(jnp.bfloat16)
            else:
                kv_ref[:, (head - heads) * HEAD:(head - heads + 1) * HEAD] = yh.astype(jnp.bfloat16)


def qkv_project(hidden, seq, gain, w, cos, sin, heads, kv_heads, rows=512):
    _, tokens, d_model = hidden.shape
    width = w.shape[1]
    q_width, kv_width = heads * HEAD, 2 * kv_heads * HEAD
    return pl.pallas_call(
        functools.partial(qkv_kernel, heads=heads, kv_heads=kv_heads),
        out_shape=(jax.ShapeDtypeStruct((tokens, q_width), jnp.bfloat16), jax.ShapeDtypeStruct((tokens, kv_width), jnp.bfloat16)),
        grid=(tokens // rows,),
        in_specs=[
            pl.BlockSpec((1, rows, d_model), lambda i: (seq, i, 0)),
            pl.BlockSpec((1, d_model), lambda i: (0, 0)),
            pl.BlockSpec((d_model, width), lambda i: (0, 0), pipeline_mode=pl.Buffered(1)),
            pl.BlockSpec((rows, HEAD), lambda i: (seq * (tokens // rows) + i, 0)),
            pl.BlockSpec((rows, HEAD), lambda i: (seq * (tokens // rows) + i, 0)),
        ],
        out_specs=(pl.BlockSpec((rows, q_width), lambda i: (i, 0)), pl.BlockSpec((rows, kv_width), lambda i: (i, 0))),
        scratch_shapes=[pltpu.VMEM((rows, d_model), jnp.bfloat16)],
        compiler_params=params(1),
        cost_estimate=cost(2 * tokens * d_model * width, 2 * tokens * d_model),
        name='qkv_project',
    )(hidden, gain, w, cos, sin)


def attn_kernel(place_ref, q_ref, k_mine, v_mine, k_peer, v_peer, o_ref, m_scr, l_scr, acc_scr, k_ref, v_ref, *, heads, seg_len, scale):
    step = pl.program_id(1)
    cp = place_ref[0]
    slot = (step >= 1 + cp).astype(jnp.int32)
    seg = step - slot * (1 + cp)
    diagonal = (step == cp) | (step == 4)
    mine = ((seg == 1) | (seg == 2)).astype(jnp.int32) == cp
    k_ref[...] = jnp.where(mine, k_mine[...], k_peer[...])
    v_ref[...] = jnp.where(mine, v_mine[...], v_peer[...])

    @pl.when(seg == 0)
    def _():
        m_scr[...] = jnp.full_like(m_scr, -jnp.inf)
        l_scr[...] = jnp.zeros_like(l_scr)
        acc_scr[...] = jnp.zeros_like(acc_scr)

    def score(h, i, width, last):
        rs = slice(i * ROWS, (i + 1) * ROWS)
        hs = slice(h * HEAD, (h + 1) * HEAD)
        return lax.dot_general(q_ref[rs, hs], k_ref[0:width, :], (((1,), (1,)), ((), ())), preferred_element_type=jnp.float32)

    def absorb(s, h, i, width, last):
        rs = slice(i * ROWS, (i + 1) * ROWS)
        hs = slice(h * HEAD, (h + 1) * HEAD)
        if last:
            row = lax.broadcasted_iota(jnp.int32, (ROWS, width), 0) + i * ROWS
            col = lax.broadcasted_iota(jnp.int32, (ROWS, width), 1)
            s = jnp.where(col <= row, s, -jnp.inf)
        m_old = m_scr[h, rs, :]
        m_new = jnp.maximum(m_old, jnp.max(s, axis=1, keepdims=True))
        alpha = jnp.exp2((m_old - m_new) * scale)
        p = jnp.exp2((s - m_new[:, :1]) * scale)
        l_new = alpha * l_scr[h, rs, :] + jnp.sum(p, axis=1, keepdims=True)
        pv = jnp.dot(p.astype(jnp.bfloat16), v_ref[0:width, :], preferred_element_type=jnp.float32)
        acc = alpha * acc_scr[rs, hs] + pv
        if last:
            o_ref[rs, hs] = (acc / l_new).astype(jnp.bfloat16)
        else:
            m_scr[h, rs, :] = m_new
            l_scr[h, rs, :] = l_new
            acc_scr[rs, hs] = acc

    def run(tiles):
        ahead = score(*tiles[0])
        for n, tile in enumerate(tiles):
            s, ahead = ahead, score(*tiles[n + 1]) if n + 1 < len(tiles) else None
            absorb(s, *tile)

    blocks = [(h, i) for h in range(heads) for i in range(seg_len // ROWS)]

    @pl.when(jnp.logical_not(diagonal))
    def _():
        run([(h, i, seg_len, False) for h, i in blocks])

    @pl.when(diagonal)
    def _():
        run([(h, i, (i + 1) * ROWS, True) for h, i in blocks])


def attention(place, q, kv, kv_peer, kv_heads):
    tokens, width = q.shape
    seg_len = tokens // 2
    group_width = width // kv_heads
    heads = group_width // HEAD

    def slot_of(step, c):
        return (step >= 1 + c).astype(jnp.int32)

    def kv_map(offset):
        def index(g, step, place):
            seg = step - slot_of(step, place[0]) * (1 + place[0])
            return seg // 2, offset + g

        return index

    q_spec = pl.BlockSpec((seg_len, group_width), lambda g, step, place: (slot_of(step, place[0]), g))
    k_spec = pl.BlockSpec((seg_len, HEAD), kv_map(0))
    v_spec = pl.BlockSpec((seg_len, HEAD), kv_map(kv_heads))
    return pl.pallas_call(
        functools.partial(attn_kernel, heads=heads, seg_len=seg_len, scale=HEAD ** -0.5 * LOG2E),
        out_shape=jax.ShapeDtypeStruct((tokens, width), jnp.bfloat16),
        grid_spec=pltpu.PrefetchScalarGridSpec(
            num_scalar_prefetch=1,
            grid=(kv_heads, 5),
            in_specs=[q_spec, k_spec, v_spec, k_spec, v_spec],
            out_specs=q_spec,
            scratch_shapes=[
                pltpu.VMEM((heads, seg_len, HEAD), jnp.float32),
                pltpu.VMEM((heads, seg_len, HEAD), jnp.float32),
                pltpu.VMEM((seg_len, group_width), jnp.float32),
                pltpu.VMEM((seg_len, HEAD), jnp.bfloat16),
                pltpu.VMEM((seg_len, HEAD), jnp.bfloat16),
            ],
        ),
        compiler_params=params(2),
        cost_estimate=cost(18 * width * seg_len * seg_len, 4 * tokens * width),
        name='attention',
    )(place, q, kv, kv, kv_peer, kv_peer)


def resid_norm_kernel(h_ref, part_ref, peer_ref, gain_ref, r_ref, b_ref):
    attn = (part_ref[...].astype(jnp.float32) + peer_ref[...].astype(jnp.float32)).astype(jnp.bfloat16)
    r16 = (h_ref[0].astype(jnp.float32) + attn.astype(jnp.float32)).astype(jnp.bfloat16)
    r_ref[...] = r16
    r = r16.astype(jnp.float32)
    mean_sq = jnp.mean(r * r, axis=-1, keepdims=True)
    b_ref[...] = (r * lax.rsqrt(mean_sq + NORM_EPS) * gain_ref[...]).astype(jnp.bfloat16)


def resid_norm(hidden, seq, part, peer, gain, rows=256):
    tokens, d_model = part.shape
    block = pl.BlockSpec((rows, d_model), lambda i: (i, 0))
    return pl.pallas_call(
        resid_norm_kernel,
        out_shape=(jax.ShapeDtypeStruct((tokens, d_model), jnp.bfloat16),) * 2,
        grid=(tokens // rows,),
        in_specs=[pl.BlockSpec((1, rows, d_model), lambda i: (seq, i, 0)), block, block, pl.BlockSpec((1, d_model), lambda i: (0, 0))],
        out_specs=(block, block),
        compiler_params=params(1),
        cost_estimate=cost(10 * tokens * d_model, 10 * tokens * d_model),
        name='resid_norm',
    )(hidden, part, peer, gain)


def gate_up_kernel(b_ref, *refs, blocks):
    u_ref = refs[-1]
    step = pl.program_id(0)
    at = 0
    for k, n in enumerate(blocks):
        @pl.when((step >= at) & (step < at + n))
        def _(wg_ref=refs[2 * k], wu_ref=refs[2 * k + 1]):
            g = jnp.dot(b_ref[...], wg_ref[...], preferred_element_type=jnp.float32)
            t = jnp.dot(b_ref[...], wu_ref[...], preferred_element_type=jnp.float32)
            u_ref[...] = (jax.nn.silu(g) * t).astype(jnp.bfloat16)

        at += n


def gate_up(b, weights, u, first, ff):
    tokens, d_model = b.shape
    blocks = tuple(w.shape[1] // (2 * F_UNIT) for w in weights)
    in_specs = [pl.BlockSpec((tokens, d_model), lambda j: (0, 0), pipeline_mode=pl.Buffered(1))]
    operands = [b]
    at = 0
    for w, n in zip(weights, blocks):
        for side in (0, n):
            in_specs.append(pl.BlockSpec((d_model, F_UNIT), lambda j, at=at, n=n, side=side: (0, side + jnp.clip(j - at, 0, n - 1))))
            operands.append(w)
        at += n
    aliases = {}
    if u is not None:
        aliases = {len(operands): 0}
        in_specs.append(pl.BlockSpec(memory_space=pl.ANY))
        operands.append(u)
    return pl.pallas_call(
        functools.partial(gate_up_kernel, blocks=blocks),
        out_shape=jax.ShapeDtypeStruct((tokens, ff), jnp.bfloat16),
        grid=(sum(blocks),),
        in_specs=in_specs,
        out_specs=pl.BlockSpec((tokens, F_UNIT), lambda j: (0, first + j)),
        input_output_aliases=aliases,
        compiler_params=params(1),
        cost_estimate=cost(4 * tokens * d_model * sum(blocks) * F_UNIT, 4 * d_model * sum(blocks) * F_UNIT),
        name='gate_up',
    )(*operands)


def down_kernel(u_ref, w0_ref, w1_ref, o_ref):
    w = jnp.concatenate([w0_ref[...], w1_ref[...]], axis=1)
    y = jnp.dot(u_ref[...], w, preferred_element_type=jnp.float32).astype(jnp.bfloat16)
    o_ref[0] = y[:, :HEAD]
    o_ref[1] = y[:, HEAD:]


def down_project(u, w0, w1, first, blocks, rows=768):
    tokens, ff = u.shape
    w_spec = pl.BlockSpec((ff, HEAD), lambda i, j: (0, first + j))
    return pl.pallas_call(
        down_kernel,
        out_shape=jax.ShapeDtypeStruct((2, tokens, blocks * HEAD), jnp.bfloat16),
        grid=(tokens // rows, blocks),
        in_specs=[pl.BlockSpec((rows, ff), lambda i, j: (i, 0)), w_spec, w_spec],
        out_specs=pl.BlockSpec((2, rows, HEAD), lambda i, j: (0, i, j)),
        compiler_params=params(2),
        cost_estimate=cost(4 * tokens * ff * blocks * HEAD, 2 * tokens * ff),
        name='down_project',
    )(u, w0, w1)


def final_kernel(place_ref, r_ref, *refs):
    n = sum(ref.shape[0] == 2 for ref in refs[:-1]) // 2
    out_ref = refs[-1]
    cp = place_ref[0]
    shard = r_ref.shape[1] // 2
    for side in range(2):
        at = side * shard
        for part_ref, peer_ref in zip(refs[:n], refs[n:2 * n]):
            width = part_ref.shape[2]
            down = (part_ref[cp ^ side].astype(jnp.float32) + peer_ref[cp ^ side].astype(jnp.float32)).astype(jnp.bfloat16)
            cs = slice(at, at + width)
            out_ref[0, :, cs] = (r_ref[:, cs].astype(jnp.float32) + down.astype(jnp.float32)).astype(jnp.bfloat16)
            at += width


def final_add(place, r, parts, peers, out, seq, half, shape, rows=768):
    tokens, d_model = r.shape
    width = d_model // 2
    piece_specs = [pl.BlockSpec((2, rows, p.shape[2]), lambda i, place: (0, i, 0)) for p in parts]
    in_specs = [pl.BlockSpec((rows, width), lambda i, place: (i, place[1] ^ half))] + piece_specs + piece_specs
    operands = [r, *parts, *peers]
    aliases = {}
    if out is not None:
        in_specs.append(pl.BlockSpec(memory_space=pl.ANY))
        operands.append(out)
        aliases = {len(operands): 0}
    return pl.pallas_call(
        final_kernel,
        out_shape=jax.ShapeDtypeStruct(shape, jnp.bfloat16),
        grid_spec=pltpu.PrefetchScalarGridSpec(
            num_scalar_prefetch=1,
            grid=(tokens // rows,),
            in_specs=in_specs,
            out_specs=pl.BlockSpec((1, rows, width), lambda i, place: (seq, i, place[1] ^ half)),
        ),
        input_output_aliases=aliases,
        compiler_params=params(1),
        cost_estimate=cost(3 * tokens * width, 10 * tokens * width),
        name='final_add',
    )(place, *operands)


def after(value, *earlier):
    return lax.optimization_barrier((value, *earlier))[0]


def solution(mesh):
    seq_spec = P(('dp', 'fsdp'), 'cp', None)
    pos_spec = P(('dp', 'fsdp'), 'cp')
    in_spec = P(GROUP_AXES, 'tp', None)
    out_spec = P('tp', None, GROUP_AXES)
    col_spec = P(GROUP_AXES, 'tp')
    row_spec = P('tp', GROUP_AXES)
    rep_spec = P(None)
    swap = [(0, 1), (1, 0)]

    def layer_local(hidden, positions, attn_gain, w_query, w_key, w_value, w_out, mlp_gain, w_gate, w_up, w_down):
        n_seqs, _, _ = hidden.shape
        heads, kv_heads = w_query.shape[1], w_key.shape[1]
        shard = w_query.shape[0]
        ff = w_gate.shape[1]

        w_qkv = jnp.concatenate([w.reshape(shard, -1) for w in (w_query, w_key, w_value)], axis=1)
        full_qkv = lax.all_gather(w_qkv, GROUP_AXES, axis=0, tiled=True)
        full_out = lax.all_gather(w_out.reshape(heads * HEAD, shard), GROUP_AXES, axis=1, tiled=True)
        full_gu, firsts, at = [], [], 0
        for n in F_CHUNKS:
            cs = slice(at * F_UNIT, (at + n) * F_UNIT)
            firsts.append(at)
            chunk = jnp.concatenate([w_gate[:, cs], w_up[:, cs]], axis=1)
            full_gu.append(lax.all_gather(chunk, GROUP_AXES, axis=0, tiled=True))
            at += n
        down_local = (w_down, lax.ppermute(w_down, 'cp', swap))
        own_chunks = [w_down[:, first * HEAD:(first + n) * HEAD] for first, n in D_CHUNKS]
        remote, down_remote = [], {}

        inv_freq = ROPE_THETA ** (-jnp.arange(0, HEAD, 2, dtype=jnp.float32) / HEAD)
        angles = positions.reshape(-1).astype(jnp.float32)[:, None] * inv_freq
        cos, sin = jnp.cos(angles), jnp.sin(angles)
        cos = jnp.concatenate([cos, cos], axis=-1)
        sin = jnp.concatenate([-sin, sin], axis=-1)
        place = jnp.stack([lax.axis_index('cp'), lax.axis_index('fsdp')]).astype(jnp.int32)

        q, kv, kv_peer, part, peer, r, b, u = ([None] * n_seqs for _ in range(8))
        d_part = {(s, half): [] for s in range(n_seqs) for half in range(2)}
        d_peer = {key: [] for key in d_part}
        out, last = None, own_chunks[0]

        def tied(value):
            return after(value, last)

        for kind, s, *rest in STEPS:
            if kind == 'q':
                q[s], kv[s] = qkv_project(tied(hidden), s, attn_gain[None], full_qkv, cos, sin, heads, kv_heads)
                last = kv[s]
            elif kind == 'a':
                last = attention(place, tied(q[s]), kv[s], kv_peer[s], kv_heads)
                part[s] = last
            elif kind == 'o':
                last = jnp.dot(tied(part[s]), full_out, preferred_element_type=jnp.float32).astype(jnp.bfloat16)
                part[s] = last
            elif kind == 'n':
                r[s], b[s] = resid_norm(hidden, s, tied(part[s]), peer[s], mlp_gain[None])
                last = b[s]
            elif kind == 'g':
                c, n = rest
                last = u[s] = gate_up(tied(b[s]), full_gu[c:c + n], u[s], firsts[c], ff)
            elif kind == 'd':
                half, first, n = rest
                if half:
                    last = down_project(tied(u[s]), *down_remote[first, n], 0, n)
                else:
                    last = down_project(tied(u[s]), *down_local, first, n)
                d_part[s, half].append(last)
            elif kind == 'f':
                half = rest[0]
                last = out = final_add(place, r[s], [tied(p) for p in d_part[s, half]], d_peer[s, half], out, s, half, hidden.shape)
            if kind == 'R':
                for chunk, columns in enumerate(own_chunks):
                    remote.append(lax.ppermute(tied(columns), 'fsdp', swap))
            if kind == 'R2':
                down_remote[D_CHUNKS[s]] = (remote[s], lax.ppermute(tied(remote[s]), 'cp', swap))
            if kind == 'q':
                kv_peer[s] = lax.ppermute(kv[s], 'cp', swap)
            elif kind == 'o':
                peer[s] = lax.ppermute(part[s], 'tp', swap)
            elif kind == 'd':
                d_peer[s, half].append(lax.ppermute(last, 'tp', swap))
        return out

    return jax.shard_map(layer_local, mesh=mesh, in_specs=(seq_spec, pos_spec, rep_spec, in_spec, in_spec, in_spec, out_spec, rep_spec, col_spec, col_spec, row_spec), out_specs=seq_spec, check_vma=False)
```

time: 4780 us -> 2330 us (0.49)
  matrix products: 1900 us -> 85 us
  Pallas kernels: 0 us -> 1610 us
  waiting for transfers between devices: 1930 us -> 514 us
  local copies, waits for them, and re-layouts: 517 us -> 47.8 us
  other arithmetic: 332 us -> 38.6 us
  loops' own time: 71.6 us -> 0 us
    dot_general x79 -> x3, matrix products: 1900 us -> 85 us  [layer_local(): jnp.dot(tied(part[s]), full_out, preferred_element_type=jnp.float32)]
    pallas_call x0 -> x35, Pallas kernels: none -> 1610 us  [the longest x10 729 us: gate_up(): pl.pallas_call(functools.partial(gate_up_kernel, blocks=blocks), out_shap...]
    psum x2 -> x0, waiting for transfers between devices: 1440 us -> none  [the longest x1 721 us: layer_local(): down_proj = lax.psum(down_part, 'tp')]
    ppermute x0 -> x21, waiting for transfers between devices: none -> 467 us  [the longest x10 327 us: layer_local(): d_peer[s, half].append(lax.ppermute(last, 'tp', swap))]
    all_gather x9 -> x6, waiting for transfers between devices: 485 us -> 46 us  [the longest x1 46 us: layer_local(): full_qkv = lax.all_gather(w_qkv, GROUP_AXES, axis=0, tiled=True)]
    while x73 -> x0, local copies, waits for them, and re-layouts: 310 us -> none
    reduce_sum x38 -> x0, other arithmetic: 209 us -> none  [the longest x36 164 us: one_block(): row_sum = jnp.sum(probs, axis=-1)]
    another operation x1 -> x0, loops' own time: 71.6 us -> none  [attention(): mixed = lax.map(one_block, (q_blocks, pos_blocks, seq_ids))]
  transfers between devices with their start and end apart: 11 -> 27, of which waited for: 6 -> 9; matrix products, arithmetic and copies ran while one was open for 42% -> 7% of each run, Pallas kernels for 0% -> 69%
where the time goes in v1:
time: 2330 us; the launch traced here: 2320 us
  Pallas kernels  1610 us (69%)
  waiting for transfers between devices  514 us (22%)
  matrix products  85 us (4%)
  local copies, waits for them, and re-layouts  47.8 us (2%)
  other arithmetic  38.6 us (2%)
    pallas_call x10, Pallas kernels, gate_up(): pl.pallas_call(functools.partial(gate_up_kernel, blocks=blocks), out_shap...  729 us
    pallas_call x10, Pallas kernels, down_project(): pl.pallas_call(down_kernel, out_shape=jax.ShapeDtypeStruct((2, tokens, bl...  435 us
    ppermute x10, waiting for transfers between devices, layer_local(): d_peer[s, half].append(lax.ppermute(last, 'tp', swap))  327 us
    pallas_call x3, Pallas kernels, attention(): pl.pallas_call(functools.partial(attn_kernel, heads=heads, seg_len=seg_le...  211 us
    pallas_call x3, Pallas kernels, qkv_project(): pl.pallas_call(functools.partial(qkv_kernel, heads=heads, kv_heads=kv_hea...  119 us
    dot_general x3, matrix products, layer_local(): jnp.dot(tied(part[s]), full_out, preferred_element_type=jnp.float32)  85 us
    ppermute x3, waiting for transfers between devices, layer_local(): peer[s] = lax.ppermute(part[s], 'tp', swap)  83.7 us
    pallas_call x3, Pallas kernels, resid_norm(): pl.pallas_call(resid_norm_kernel, out_shape=(jax.ShapeDtypeStruct((tokens...  60.3 us
  transfers between devices with their start and end apart: 27, of which 9 were waited for; matrix products, arithmetic and copies ran while one was open for 7% of the time, Pallas kernels for 69%

profile of v1, /device:TPU:0, one launch (start us, length us, event | category | flops | bytes accessed | tf_op | source)
XLA Modules:
  0.0 2323.8 jit_solution(6895899950859785493)
XLA Ops:
  78.2 46.0 %all-gather.7.cloned.1.call-done.w_ref = bf16[3584,2304]{1,0:T(8,128)(2,1)} async-done(((bf16[896,2304]{1,0:T(8,128)(2,1)}), bf16[3584,2304]{1,0:T(8,128)(2,1)}) %all-gather.7.cloned.1.call-update) | async-done | bytes 16515088 | tf_op jit(solution)/shard_map/all_gather | solution.py:341
  124.2 40.4 %qkv_project.3 = (bf16[1536,1792]{1,0:T(8,128)(2,1)}, bf16[1536,512]{1,0:T(8,128)(2,1)}) custom-call(bf16[3,1536,3584]{2,1,0:T(8,128)(2,1)} %h_ref.5, f32[1,3584]{1,0:T(1,128)} %broadcast_in_dim.4.gain_ref, bf16[3584,2304]{1,0:T(8,128)(2,1)} %all-gather.7.cloned.1.call-done.w_ref, f32[4608,128]{1,0:T(8,128)} %get-tuple-element.127.cos_ref, ...), custom_call_target="tpu_custom_call" | custom-call | flops 25367150592 | bytes 11010048 | tf_op jit(solution)/shard_map/qkv_project/pallas_call | solution.py:70
  181.4 70.4 %attention.3 = bf16[1536,1792]{1,0:T(8,128)(2,1)} custom-call(s32[2]{0:T(128)} %pad_add_fusion.place_ref, bf16[1536,1792]{1,0:T(8,128)(2,1)} %get-tuple-element.62.q_ref, bf16[1536,512]{1,0:T(8,128)(2,1)} %get-tuple-element.63.k_mine.v_mine, bf16[1536,512]{1,0:T(8,128)(2,1)} %get-tuple-element.63.k_mine.v_mine, ...), custom_call_target="tpu_custom_call" | custom-call | flops 19025362944 | bytes 11010048 | tf_op jit(solution)/shard_map/attention/pallas_call | solution.py:167
  279.4 39.2 %qkv_project.4 = (bf16[1536,1792]{1,0:T(8,128)(2,1)}, bf16[1536,512]{1,0:T(8,128)(2,1)}) custom-call(bf16[3,1536,3584]{2,1,0:T(8,128)(2,1)} %h_ref.5, f32[1,3584]{1,0:T(1,128)} %broadcast_in_dim.4.gain_ref, bf16[3584,2304]{1,0:T(8,128)(2,1)} %all-gather.7.cloned.1.call-done.w_ref, f32[4608,128]{1,0:T(8,128)} %get-tuple-element.127.cos_ref, ...), custom_call_target="tpu_custom_call" | custom-call | flops 25367150592 | bytes 11010048 | tf_op jit(solution)/shard_map/qkv_project/pallas_call | solution.py:70
  320.1 39.1 %qkv_project.5 = (bf16[1536,1792]{1,0:T(8,128)(2,1)}, bf16[1536,512]{1,0:T(8,128)(2,1)}) custom-call(bf16[3,1536,3584]{2,1,0:T(8,128)(2,1)} %h_ref.5, f32[1,3584]{1,0:T(1,128)} %broadcast_in_dim.4.gain_ref, bf16[3584,2304]{1,0:T(8,128)(2,1)} %all-gather.7.cloned.1.call-done.w_ref, f32[4608,128]{1,0:T(8,128)} %get-tuple-element.127.cos_ref, ...), custom_call_target="tpu_custom_call" | custom-call | flops 25367150592 | bytes 11010048 | tf_op jit(solution)/shard_map/qkv_project/pallas_call | solution.py:70
  359.2 70.0 %attention.4 = bf16[1536,1792]{1,0:T(8,128)(2,1)} custom-call(s32[2]{0:T(128)} %pad_add_fusion.place_ref, bf16[1536,1792]{1,0:T(8,128)(2,1)} %get-tuple-element.70.q_ref, bf16[1536,512]{1,0:T(8,128)(2,1)} %get-tuple-element.65.k_mine.v_mine, bf16[1536,512]{1,0:T(8,128)(2,1)} %get-tuple-element.65.k_mine.v_mine, ...), custom_call_target="tpu_custom_call" | custom-call | flops 19025362944 | bytes 11010048 | tf_op jit(solution)/shard_map/attention/pallas_call | solution.py:167
  429.2 30.3 %convolution_convert_fusion.1.part_ref = bf16[1536,3584]{1,0:T(8,128)(2,1)} fusion(bf16[1536,1792]{1,0:T(8,128)(2,1)} %attention.4, bf16[1792,3584]{1,0:T(8,128)(2,1)} %all-gather.9.cloned.1.call-done), kind=kOutput, calls=%fused_computation.1 | convolution fusion | flops 19735511040 | bytes 29360128 | tf_op jit(solution)/shard_map/dot_general | solution.py:377
  459.6 70.4 %attention.5 = bf16[1536,1792]{1,0:T(8,128)(2,1)} custom-call(s32[2]{0:T(128)} %pad_add_fusion.place_ref, bf16[1536,1792]{1,0:T(8,128)(2,1)} %get-tuple-element.71.q_ref, bf16[1536,512]{1,0:T(8,128)(2,1)} %get-tuple-element.69.k_mine.v_mine, bf16[1536,512]{1,0:T(8,128)(2,1)} %get-tuple-element.69.k_mine.v_mine, ...), custom_call_target="tpu_custom_call" | custom-call | flops 19025362944 | bytes 11010048 | tf_op jit(solution)/shard_map/attention/pallas_call | solution.py:167
  607.2 65.6 %gate_up.10.refs_2_ = bf16[1536,9472]{1,0:T(8,128)(2,1)} custom-call(bf16[1536,3584]{1,0:T(8,128)(2,1)} %get-tuple-element.88.b_ref, bf16[3584,5120]{1,0:T(8,128)(2,1)} %all-gather.11.cloned.1.call-done.refs_0_.refs_1_, bf16[3584,5120]{1,0:T(8,128)(2,1)} %all-gather.11.cloned.1.call-done.refs_0_.refs_1_), custom_call_target="tpu_custom_call" | custom-call | flops 56371445760 | bytes 36700160 | tf_op jit(solution)/shard_map/gate_up/pallas_call | solution.py:243
  672.7 66.6 %gate_up.11.refs_2_ = bf16[1536,9472]{1,0:T(8,128)(2,1)} custom-call(bf16[1536,3584]{1,0:T(8,128)(2,1)} %get-tuple-element.88.b_ref, bf16[3584,5120]{1,0:T(8,128)(2,1)} %all-gather.13.cloned.1.call-done.refs_0_.refs_1_.refs_2_.refs_3_, ...), custom_call_target="tpu_custom_call", output_to_operand_aliasing={{}: (3, {})} | custom-call | flops 56371445760 | bytes 36700160 | tf_op jit(solution)/shard_map/gate_up/pallas_call | solution.py:243
  739.3 55.2 %collective-permute-done.4.peer_ref = bf16[1536,3584]{1,0:T(8,128)(2,1)} collective-permute-done((bf16[1536,3584]{1,0:T(8,128)(2,1)}, bf16[1536,3584]{1,0:T(8,128)(2,1)}, u32[]{:S(2)}, u32[]{:S(2)}) %collective-permute-start.4) | collective-permute-done | bytes 11010080 | tf_op jit(solution)/shard_map/ppermute | solution.py:403
  814.6 127.9 %gate_up.12.refs_2_ = bf16[1536,9472]{1,0:T(8,128)(2,1)} custom-call(bf16[1536,3584]{1,0:T(8,128)(2,1)} %get-tuple-element.85.b_ref, bf16[3584,5120]{1,0:T(8,128)(2,1)} %all-gather.11.cloned.1.call-done.refs_0_.refs_1_, bf16[3584,5120]{1,0:T(8,128)(2,1)} %all-gather.11.cloned.1.call-done.refs_0_.refs_1_, ...), custom_call_target="tpu_custom_call" | custom-call | flops 112742891520 | bytes 73400320 | tf_op jit(solution)/shard_map/gate_up/pallas_call | solution.py:243
  942.5 66.0 %gate_up.13.refs_2_ = bf16[1536,9472]{1,0:T(8,128)(2,1)} custom-call(bf16[1536,3584]{1,0:T(8,128)(2,1)} %get-tuple-element.88.b_ref, bf16[3584,5120]{1,0:T(8,128)(2,1)} %all-gather.15.cloned.1.call-done.refs_0_.refs_1_, bf16[3584,5120]{1,0:T(8,128)(2,1)} %all-gather.15.cloned.1.call-done.refs_0_.refs_1_, ...), custom_call_target="tpu_custom_call", output_to_operand_aliasing={{}: (3, {})} | custom-call | flops 56371445760 | bytes 36700160 | tf_op jit(solution)/shard_map/gate_up/pallas_call | solution.py:243
  1008.5 65.5 %gate_up.14.refs_2_ = bf16[1536,9472]{1,0:T(8,128)(2,1)} custom-call(bf16[1536,3584]{1,0:T(8,128)(2,1)} %get-tuple-element.85.b_ref, bf16[3584,5120]{1,0:T(8,128)(2,1)} %all-gather.15.cloned.1.call-done.refs_0_.refs_1_, bf16[3584,5120]{1,0:T(8,128)(2,1)} %all-gather.15.cloned.1.call-done.refs_0_.refs_1_, ...), custom_call_target="tpu_custom_call", output_to_operand_aliasing={{}: (3, {})} | custom-call | flops 56371445760 | bytes 36700160 | tf_op jit(solution)/shard_map/gate_up/pallas_call | solution.py:243
  1094.1 47.9 %gate_up.15.u_ref = bf16[1536,9472]{1,0:T(8,128)(2,1)} custom-call(bf16[1536,3584]{1,0:T(8,128)(2,1)} %get-tuple-element.85.b_ref, bf16[3584,3584]{1,0:T(8,128)(2,1)} %all-gather.17.cloned.1.call-done.refs_0_.refs_1_.refs_2_.refs_3_, bf16[3584,3584]{1,0:T(8,128)(2,1)} %all-gather.17.cloned.1.call-done.refs_0_.refs_1_.refs_2_.refs_3_, ...), custom_call_target="tpu_custom_call", output_to_operand_aliasing={{}: (3, {})} | custom-call | flops 39460012032 | bytes 25690112 | tf_op jit(solution)/shard_map/gate_up/pallas_call | solution.py:243
  1142.0 65.7 %down_project.10.refs_0_ = bf16[2,1536,896]{2,1,0:T(8,128)(2,1)} custom-call(bf16[1536,9472]{1,0:T(8,128)(2,1)} %gate_up.15.u_ref, bf16[9472,896]{1,0:T(8,128)(2,1)} %w0_ref.7, bf16[9472,896]{1,0:T(8,128)(2,1)} %collective-permute-done.6.w1_ref), custom_call_target="tpu_custom_call" | custom-call | flops 52143587328 | bytes 29097984 | tf_op jit(solution)/shard_map/down_project/pallas_call | solution.py:266
  1207.6 65.6 %gate_up.16.refs_2_ = bf16[1536,9472]{1,0:T(8,128)(2,1)} custom-call(bf16[1536,3584]{1,0:T(8,128)(2,1)} %get-tuple-element.99.b_ref, bf16[3584,5120]{1,0:T(8,128)(2,1)} %all-gather.11.cloned.1.call-done.refs_0_.refs_1_, bf16[3584,5120]{1,0:T(8,128)(2,1)} %all-gather.11.cloned.1.call-done.refs_0_.refs_1_), custom_call_target="tpu_custom_call" | custom-call | flops 56371445760 | bytes 36700160 | tf_op jit(solution)/shard_map/gate_up/pallas_call | solution.py:243
  1300.0 48.0 %gate_up.17.u_ref = bf16[1536,9472]{1,0:T(8,128)(2,1)} custom-call(bf16[1536,3584]{1,0:T(8,128)(2,1)} %get-tuple-element.88.b_ref, bf16[3584,3584]{1,0:T(8,128)(2,1)} %all-gather.17.cloned.1.call-done.refs_0_.refs_1_.refs_2_.refs_3_, bf16[3584,3584]{1,0:T(8,128)(2,1)} %all-gather.17.cloned.1.call-done.refs_0_.refs_1_.refs_2_.refs_3_, ...), custom_call_target="tpu_custom_call", output_to_operand_aliasing={{}: (3, {})} | custom-call | flops 39460012032 | bytes 25690112 | tf_op jit(solution)/shard_map/gate_up/pallas_call | solution.py:243
  1348.0 33.9 %down_project.11.refs_0_ = bf16[2,1536,384]{2,1,0:T(8,128)(2,1)} custom-call(bf16[1536,9472]{1,0:T(8,128)(2,1)} %gate_up.15.u_ref, bf16[9472,384]{1,0:T(8,128)(2,1)} %collective-permute-done.7.w0_ref, bf16[9472,384]{1,0:T(8,128)(2,1)} %collective-permute-done.8.w1_ref), custom_call_target="tpu_custom_call" | custom-call | flops 22347251712 | bytes 29097984 | tf_op jit(solution)/shard_map/down_project/pallas_call | solution.py:266
  1381.9 33.9 %down_project.12.refs_0_ = bf16[2,1536,384]{2,1,0:T(8,128)(2,1)} custom-call(bf16[1536,9472]{1,0:T(8,128)(2,1)} %gate_up.17.u_ref, bf16[9472,384]{1,0:T(8,128)(2,1)} %collective-permute-done.7.w0_ref, bf16[9472,384]{1,0:T(8,128)(2,1)} %collective-permute-done.8.w1_ref), custom_call_target="tpu_custom_call" | custom-call | flops 22347251712 | bytes 29097984 | tf_op jit(solution)/shard_map/down_project/pallas_call | solution.py:266
  1415.8 65.6 %down_project.13.refs_0_ = bf16[2,1536,896]{2,1,0:T(8,128)(2,1)} custom-call(bf16[1536,9472]{1,0:T(8,128)(2,1)} %gate_up.17.u_ref, bf16[9472,896]{1,0:T(8,128)(2,1)} %w0_ref.7, bf16[9472,896]{1,0:T(8,128)(2,1)} %collective-permute-done.6.w1_ref), custom_call_target="tpu_custom_call" | custom-call | flops 52143587328 | bytes 29097984 | tf_op jit(solution)/shard_map/down_project/pallas_call | solution.py:266
  1513.9 66.0 %gate_up.18.refs_4_ = bf16[1536,9472]{1,0:T(8,128)(2,1)} custom-call(bf16[1536,3584]{1,0:T(8,128)(2,1)} %get-tuple-element.99.b_ref, bf16[3584,5120]{1,0:T(8,128)(2,1)} %all-gather.13.cloned.1.call-done.refs_0_.refs_1_.refs_2_.refs_3_, ...), custom_call_target="tpu_custom_call", output_to_operand_aliasing={{}: (3, {})} | custom-call | flops 56371445760 | bytes 36700160 | tf_op jit(solution)/shard_map/gate_up/pallas_call | solution.py:243
  1579.9 41.9 %down_project.14.refs_1_ = bf16[2,1536,512]{2,1,0:T(8,128)(2,1)} custom-call(bf16[1536,9472]{1,0:T(8,128)(2,1)} %gate_up.17.u_ref, bf16[9472,512]{1,0:T(8,128)(2,1)} %collective-permute-done.9.w0_ref, bf16[9472,512]{1,0:T(8,128)(2,1)} %collective-permute-done.10.w1_ref), custom_call_target="tpu_custom_call" | custom-call | flops 29796335616 | bytes 29097984 | tf_op jit(solution)/shard_map/down_project/pallas_call | solution.py:266
  1621.8 41.9 %down_project.15.refs_1_ = bf16[2,1536,512]{2,1,0:T(8,128)(2,1)} custom-call(bf16[1536,9472]{1,0:T(8,128)(2,1)} %gate_up.15.u_ref, bf16[9472,512]{1,0:T(8,128)(2,1)} %collective-permute-done.9.w0_ref, bf16[9472,512]{1,0:T(8,128)(2,1)} %collective-permute-done.10.w1_ref), custom_call_target="tpu_custom_call" | custom-call | flops 29796335616 | bytes 29097984 | tf_op jit(solution)/shard_map/down_project/pallas_call | solution.py:266
  1663.7 109.6 %gate_up.19.u_ref = bf16[1536,9472]{1,0:T(8,128)(2,1)} custom-call(bf16[1536,3584]{1,0:T(8,128)(2,1)} %get-tuple-element.99.b_ref, bf16[3584,5120]{1,0:T(8,128)(2,1)} %all-gather.15.cloned.1.call-done.refs_0_.refs_1_, bf16[3584,5120]{1,0:T(8,128)(2,1)} %all-gather.15.cloned.1.call-done.refs_0_.refs_1_, ...), custom_call_target="tpu_custom_call", output_to_operand_aliasing={{}: (5, {})} | custom-call | flops 95831457792 | bytes 62390272 | tf_op jit(solution)/shard_map/gate_up/pallas_call | solution.py:243
  1799.4 34.1 %down_project.17.refs_0_ = bf16[2,1536,384]{2,1,0:T(8,128)(2,1)} custom-call(bf16[1536,9472]{1,0:T(8,128)(2,1)} %gate_up.19.u_ref, bf16[9472,384]{1,0:T(8,128)(2,1)} %collective-permute-done.7.w0_ref, bf16[9472,384]{1,0:T(8,128)(2,1)} %collective-permute-done.8.w1_ref), custom_call_target="tpu_custom_call" | custom-call | flops 22347251712 | bytes 29097984 | tf_op jit(solution)/shard_map/down_project/pallas_call | solution.py:266
  1833.5 49.8 %down_project.18.refs_1_ = bf16[2,1536,640]{2,1,0:T(8,128)(2,1)} custom-call(bf16[1536,9472]{1,0:T(8,128)(2,1)} %gate_up.19.u_ref, bf16[9472,896]{1,0:T(8,128)(2,1)} %w0_ref.7, bf16[9472,896]{1,0:T(8,128)(2,1)} %collective-permute-done.6.w1_ref), custom_call_target="tpu_custom_call" | custom-call | flops 37245419520 | bytes 29097984 | tf_op jit(solution)/shard_map/down_project/pallas_call | solution.py:266
  1896.8 41.9 %down_project.19.refs_1_ = bf16[2,1536,512]{2,1,0:T(8,128)(2,1)} custom-call(bf16[1536,9472]{1,0:T(8,128)(2,1)} %gate_up.19.u_ref, bf16[9472,512]{1,0:T(8,128)(2,1)} %collective-permute-done.9.w0_ref, bf16[9472,512]{1,0:T(8,128)(2,1)} %collective-permute-done.10.w1_ref), custom_call_target="tpu_custom_call" | custom-call | flops 29796335616 | bytes 29097984 | tf_op jit(solution)/shard_map/down_project/pallas_call | solution.py:266
  1939.8 65.4 %collective-permute-done.12.refs_2_ = bf16[2,1536,256]{2,1,0:T(8,128)(2,1)} collective-permute-done((bf16[2,1536,256]{2,1,0:T(8,128)(2,1)}, bf16[2,1536,256]{2,1,0:T(8,128)(2,1)}, u32[]{:S(2)}, u32[]{:S(2)}) %collective-permute-start.12) | collective-permute-done | bytes 1572896 | tf_op jit(solution)/shard_map/ppermute | solution.py:405
  2026.1 46.5 %collective-permute-done.16.refs_3_ = bf16[2,1536,512]{2,1,0:T(8,128)(2,1)} collective-permute-done((bf16[2,1536,512]{2,1,0:T(8,128)(2,1)}, bf16[2,1536,512]{2,1,0:T(8,128)(2,1)}, u32[]{:S(2)}, u32[]{:S(2)}) %collective-permute-start.16) | collective-permute-done | bytes 3145760 | tf_op jit(solution)/shard_map/ppermute | solution.py:405
  2082.3 175.6 %collective-permute-done.17.refs_2_ = bf16[2,1536,384]{2,1,0:T(8,128)(2,1)} collective-permute-done((bf16[2,1536,384]{2,1,0:T(8,128)(2,1)}, bf16[2,1536,384]{2,1,0:T(8,128)(2,1)}, u32[]{:S(2)}, u32[]{:S(2)}) %collective-permute-start.17) | collective-permute-done | bytes 2359328 | tf_op jit(solution)/shard_map/ppermute | solution.py:405
  2267.4 39.7 %collective-permute-done.19.refs_2_ = bf16[2,1536,384]{2,1,0:T(8,128)(2,1)} collective-permute-done((bf16[2,1536,384]{2,1,0:T(8,128)(2,1)}, bf16[2,1536,384]{2,1,0:T(8,128)(2,1)}, u32[]{:S(2)}, u32[]{:S(2)}) %collective-permute-start.19) | collective-permute-done | bytes 2359328 | tf_op jit(solution)/shard_map/ppermute | solution.py:405
  (95 shorter events, 384.4 us)
Async XLA Ops:
  6.5 117.7 %all-gather.7.cloned.1.call-start = ((), (), s32[]{:S(2)}) async-start(), calls=%async_computation | async-start | bytes 20643840 | tf_op jit(solution)/shard_map/all_gather | solution.py:341
  19.6 232.2 %all-gather.9.cloned.1.call-start = ((), (), s32[]{:S(2)}) async-start(), calls=%async_computation.1 | async-start | bytes 16056320 | tf_op jit(solution)/shard_map/all_gather | solution.py:342
  20.4 586.8 %all-gather.11.cloned.1.call-start = ((), (), s32[]{:S(2)}) async-start(), calls=%async_computation.2 | async-start | bytes 45875200 | tf_op jit(solution)/shard_map/all_gather | solution.py:348
  43.1 629.6 %all-gather.13.cloned.1.call-start = ((), (), s32[]{:S(2)}) async-start(), calls=%async_computation.3 | async-start | bytes 45875200 | tf_op jit(solution)/shard_map/all_gather | solution.py:348
  50.8 891.7 %all-gather.15.cloned.1.call-start = ((), (), s32[]{:S(2)}) async-start(), calls=%async_computation.4 | async-start | bytes 45875200 | tf_op jit(solution)/shard_map/all_gather | solution.py:348
  58.4 7.2 copy-start.1
  58.4 7.8 copy-start
  58.5 1035.6 %all-gather.17.cloned.1.call-start = ((), (), s32[]{:S(2)}) async-start(), calls=%async_computation.5 | async-start | bytes 32112640 | tf_op jit(solution)/shard_map/all_gather | solution.py:348
  164.6 1.9 slice-start
  164.6 3.0 slice-start.1
  164.6 16.8 collective-permute-start
  164.8 977.2 %collective-permute-start.6 = (bf16[9472,896]{1,0:T(8,128)(2,1)}, bf16[9472,896]{1,0:T(8,128)(2,1)}, u32[]{:S(2)}, u32[]{:S(2)}) collective-permute-start(bf16[9472,896]{1,0:T(8,128)(2,1)} %w0_ref.7), channel_id=1, source_target_pairs={{0,1},{1,0},{2,3},{3,2},{4,5},{5,4},{6,7},{7,6}} | collective-permute-start | bytes 50921480 | tf_op jit(solution)/shard_map/ppermute | solution.py:350
  170.9 9.3 copy-start.2
  318.5 40.7 %collective-permute-start.1 = (bf16[1536,512]{1,0:T(8,128)(2,1)}, bf16[1536,512]{1,0:T(8,128)(2,1)}, u32[]{:S(2)}, u32[]{:S(2)}) collective-permute-start(bf16[1536,512]{1,0:T(8,128)(2,1)} %get-tuple-element.65.k_mine.v_mine), channel_id=1, source_target_pairs={{0,1},{1,0},{2,3},{3,2},{4,5},{5,4},{6,7},{7,6}} | collective-permute-start | bytes 4718600 | tf_op jit(solution)/shard_map/ppermute | solution.py:401
  318.7 239.8 %collective-permute-start.3 = (bf16[1536,3584]{1,0:T(8,128)(2,1)}, bf16[1536,3584]{1,0:T(8,128)(2,1)}, u32[]{:S(2)}, u32[]{:S(2)}) collective-permute-start(bf16[1536,3584]{1,0:T(8,128)(2,1)} %convolution_convert_fusion.2.part_ref), channel_id=1, source_target_pairs={{0,4},{4,0},{1,5},{5,1},{2,6},{6,2},{3,7},{7,3}} | collective-permute-start | bytes 33030152 | tf_op jit(solution)/shard_map/ppermute | solution.py:403
  359.2 100.4 %collective-permute-start.2 = (bf16[1536,512]{1,0:T(8,128)(2,1)}, bf16[1536,512]{1,0:T(8,128)(2,1)}, u32[]{:S(2)}, u32[]{:S(2)}) collective-permute-start(bf16[1536,512]{1,0:T(8,128)(2,1)} %get-tuple-element.69.k_mine.v_mine), channel_id=1, source_target_pairs={{0,1},{1,0},{2,3},{3,2},{4,5},{5,4},{6,7},{7,6}} | collective-permute-start | bytes 4718600 | tf_op jit(solution)/shard_map/ppermute | solution.py:401
  459.6 334.9 %collective-permute-start.4 = (bf16[1536,3584]{1,0:T(8,128)(2,1)}, bf16[1536,3584]{1,0:T(8,128)(2,1)}, u32[]{:S(2)}, u32[]{:S(2)}) collective-permute-start(bf16[1536,3584]{1,0:T(8,128)(2,1)} %convolution_convert_fusion.1.part_ref), channel_id=1, source_target_pairs={{0,4},{4,0},{1,5},{5,1},{2,6},{6,2},{3,7},{7,3}} | collective-permute-start | bytes 33030152 | tf_op jit(solution)/shard_map/ppermute | solution.py:403
  605.8 468.2 %collective-permute-start.5 = (bf16[1536,3584]{1,0:T(8,128)(2,1)}, bf16[1536,3584]{1,0:T(8,128)(2,1)}, u32[]{:S(2)}, u32[]{:S(2)}) collective-permute-start(bf16[1536,3584]{1,0:T(8,128)(2,1)} %convolution_convert_fusion.part_ref), channel_id=1, source_target_pairs={{0,4},{4,0},{1,5},{5,1},{2,6},{6,2},{3,7},{7,3}} | collective-permute-start | bytes 33030152 | tf_op jit(solution)/shard_map/ppermute | solution.py:403
  1142.0 157.7 %collective-permute-start.7 = (bf16[9472,384]{1,0:T(8,128)(2,1)}, bf16[9472,384]{1,0:T(8,128)(2,1)}, u32[]{:S(2)}, u32[]{:S(2)}) collective-permute-start(bf16[9472,384]{1,0:T(8,128)(2,1)} %slice.30), channel_id=1, source_target_pairs={{0,2},{2,0},{1,3},{3,1},{4,6},{6,4},{5,7},{7,5}} | collective-permute-start | bytes 21823496 | tf_op jit(solution)/shard_map/ppermute | solution.py:397
  1299.7 48.3 %collective-permute-start.8 = (bf16[9472,384]{1,0:T(8,128)(2,1)}, bf16[9472,384]{1,0:T(8,128)(2,1)}, u32[]{:S(2)}, u32[]{:S(2)}) collective-permute-start(bf16[9472,384]{1,0:T(8,128)(2,1)} %collective-permute-done.7.w0_ref), channel_id=1, source_target_pairs={{0,1},{1,0},{2,3},{3,2},{4,5},{5,4},{6,7},{7,6}} | collective-permute-start | bytes 21823496 | tf_op jit(solution)/shard_map/ppermute | solution.py:399
  1299.7 211.3 %collective-permute-start.9 = (bf16[9472,512]{1,0:T(8,128)(2,1)}, bf16[9472,512]{1,0:T(8,128)(2,1)}, u32[]{:S(2)}, u32[]{:S(2)}) collective-permute-start(bf16[9472,512]{1,0:T(8,128)(2,1)} %slice.39), channel_id=1, source_target_pairs={{0,2},{2,0},{1,3},{3,1},{4,6},{6,4},{5,7},{7,5}} | collective-permute-start | bytes 29097992 | tf_op jit(solution)/shard_map/ppermute | solution.py:397
  1511.0 69.0 %collective-permute-start.10 = (bf16[9472,512]{1,0:T(8,128)(2,1)}, bf16[9472,512]{1,0:T(8,128)(2,1)}, u32[]{:S(2)}, u32[]{:S(2)}) collective-permute-start(bf16[9472,512]{1,0:T(8,128)(2,1)} %collective-permute-done.9.w0_ref), channel_id=1, source_target_pairs={{0,1},{1,0},{2,3},{3,2},{4,5},{5,4},{6,7},{7,6}} | collective-permute-start | bytes 29097992 | tf_op jit(solution)/shard_map/ppermute | solution.py:399
  1511.0 374.3 %collective-permute-start.11 = (bf16[2,1536,896]{2,1,0:T(8,128)(2,1)}, bf16[2,1536,896]{2,1,0:T(8,128)(2,1)}, u32[]{:S(2)}, u32[]{:S(2)}) collective-permute-start(bf16[2,1536,896]{2,1,0:T(8,128)(2,1)} %down_project.10.refs_0_), channel_id=1, source_target_pairs={{0,4},{4,0},{1,5},{5,1},{2,6},{6,2},{3,7},{7,3}} | collective-permute-start | bytes 16515080 | tf_op jit(solution)/shard_map/ppermute | solution.py:405
  1511.9 426.8 %collective-permute-start.14 = (bf16[2,1536,896]{2,1,0:T(8,128)(2,1)}, bf16[2,1536,896]{2,1,0:T(8,128)(2,1)}, u32[]{:S(2)}, u32[]{:S(2)}) collective-permute-start(bf16[2,1536,896]{2,1,0:T(8,128)(2,1)} %down_project.13.refs_0_), channel_id=1, source_target_pairs={{0,4},{4,0},{1,5},{5,1},{2,6},{6,2},{3,7},{7,3}} | collective-permute-start | bytes 16515080 | tf_op jit(solution)/shard_map/ppermute | solution.py:405
  1513.0 382.9 %collective-permute-start.15 = (bf16[2,1536,384]{2,1,0:T(8,128)(2,1)}, bf16[2,1536,384]{2,1,0:T(8,128)(2,1)}, u32[]{:S(2)}, u32[]{:S(2)}) collective-permute-start(bf16[2,1536,384]{2,1,0:T(8,128)(2,1)} %down_project.12.refs_0_), channel_id=1, source_target_pairs={{0,4},{4,0},{1,5},{5,1},{2,6},{6,2},{3,7},{7,3}} | collective-permute-start | bytes 7077896 | tf_op jit(solution)/shard_map/ppermute | solution.py:405
  1883.3 123.0 %collective-permute-start.13 = (bf16[2,1536,640]{2,1,0:T(8,128)(2,1)}, bf16[2,1536,640]{2,1,0:T(8,128)(2,1)}, u32[]{:S(2)}, u32[]{:S(2)}) collective-permute-start(bf16[2,1536,640]{2,1,0:T(8,128)(2,1)} %down_project.18.refs_1_), channel_id=1, source_target_pairs={{0,4},{4,0},{1,5},{5,1},{2,6},{6,2},{3,7},{7,3}} | collective-permute-start | bytes 11796488 | tf_op jit(solution)/shard_map/ppermute | solution.py:405
  1884.4 120.7 %collective-permute-start.12 = (bf16[2,1536,256]{2,1,0:T(8,128)(2,1)}, bf16[2,1536,256]{2,1,0:T(8,128)(2,1)}, u32[]{:S(2)}, u32[]{:S(2)}) collective-permute-start(bf16[2,1536,256]{2,1,0:T(8,128)(2,1)} %down_project.16.refs_0_), channel_id=1, source_target_pairs={{0,4},{4,0},{1,5},{5,1},{2,6},{6,2},{3,7},{7,3}} | collective-permute-start | bytes 4718600 | tf_op jit(solution)/shard_map/ppermute | solution.py:405
  1885.3 187.2 %collective-permute-start.16 = (bf16[2,1536,512]{2,1,0:T(8,128)(2,1)}, bf16[2,1536,512]{2,1,0:T(8,128)(2,1)}, u32[]{:S(2)}, u32[]{:S(2)}) collective-permute-start(bf16[2,1536,512]{2,1,0:T(8,128)(2,1)} %down_project.14.refs_1_), channel_id=1, source_target_pairs={{0,4},{4,0},{1,5},{5,1},{2,6},{6,2},{3,7},{7,3}} | collective-permute-start | bytes 9437192 | tf_op jit(solution)/shard_map/ppermute | solution.py:405
  1895.9 362.1 %collective-permute-start.18 = (bf16[2,1536,512]{2,1,0:T(8,128)(2,1)}, bf16[2,1536,512]{2,1,0:T(8,128)(2,1)}, u32[]{:S(2)}, u32[]{:S(2)}) collective-permute-start(bf16[2,1536,512]{2,1,0:T(8,128)(2,1)} %down_project.15.refs_1_), channel_id=1, source_target_pairs={{0,4},{4,0},{1,5},{5,1},{2,6},{6,2},{3,7},{7,3}} | collective-permute-start | bytes 9437192 | tf_op jit(solution)/shard_map/ppermute | solution.py:405
  1938.6 368.5 %collective-permute-start.20 = (bf16[2,1536,512]{2,1,0:T(8,128)(2,1)}, bf16[2,1536,512]{2,1,0:T(8,128)(2,1)}, u32[]{:S(2)}, u32[]{:S(2)}) collective-permute-start(bf16[2,1536,512]{2,1,0:T(8,128)(2,1)} %down_project.19.refs_1_), channel_id=1, source_target_pairs={{0,4},{4,0},{1,5},{5,1},{2,6},{6,2},{3,7},{7,3}} | collective-permute-start | bytes 9437192 | tf_op jit(solution)/shard_map/ppermute | solution.py:405
  2005.1 252.8 %collective-permute-start.17 = (bf16[2,1536,384]{2,1,0:T(8,128)(2,1)}, bf16[2,1536,384]{2,1,0:T(8,128)(2,1)}, u32[]{:S(2)}, u32[]{:S(2)}) collective-permute-start(bf16[2,1536,384]{2,1,0:T(8,128)(2,1)} %down_project.11.refs_0_), channel_id=1, source_target_pairs={{0,4},{4,0},{1,5},{5,1},{2,6},{6,2},{3,7},{7,3}} | collective-permute-start | bytes 7077896 | tf_op jit(solution)/shard_map/ppermute | solution.py:405
  2006.2 300.9 %collective-permute-start.19 = (bf16[2,1536,384]{2,1,0:T(8,128)(2,1)}, bf16[2,1536,384]{2,1,0:T(8,128)(2,1)}, u32[]{:S(2)}, u32[]{:S(2)}) collective-permute-start(bf16[2,1536,384]{2,1,0:T(8,128)(2,1)} %down_project.17.refs_0_), channel_id=1, source_target_pairs={{0,4},{4,0},{1,5},{5,1},{2,6},{6,2},{3,7},{7,3}} | collective-permute-start | bytes 7077896 | tf_op jit(solution)/shard_map/ppermute | solution.py:405
Sparse Core Ops, SparseCore 0:
  19.8 104.4 all-gather.6
  125.7 80.6 all-gather.8
  208.0 218.5 all-gather.10
  428.1 218.5 all-gather.12
  648.1 218.5 all-gather.14
  868.2 154.8 all-gather.16
